TPU v7x, 32 devices: a whole 2x2x4 slice. The times are simulated.
32 devices in a mesh: parts: 2 (over x), genes: 8 (over z, y), samples: 2 (over core).
Axes of the slice: x: 2, y: 2, z: 4, core: 2. Of those that a mesh axis runs over, the one named last changes fastest.
Arguments:
- dosage: bfloat16 [32768, 2048], P(('parts', 'genes'), 'samples'), parts along dimension 0, may hold values from -6 to 6
- expression: bfloat16 [128, 2048], P(('parts', 'genes'), 'samples'), parts along dimension 0, may hold values from -6 to 6
- intron_counts: bfloat16 [4096, 2560], P(('parts', 'samples', 'genes')), parts along dimension 0, may hold values from 1 to 100
- cluster_sizes: int32 [128, 8], P('parts'), parts along dimension 0, may hold values from 1 to 12, 40 in all within a row
- valid_mask: int32 [128, 40], P('parts'), parts along dimension 0, may hold values 0 or 1
- gene_block: int32 [128], P('parts'), parts along dimension 0, may hold values from 0 to 63, each once
- window_start: int32 [128], P(('parts', 'genes')), parts along dimension 0, may hold values from 0 to 1024, as said below
Outputs:
- assoc: bfloat16 [128, 41, 2048], P(('parts', 'genes'), None, 'samples'), parts along dimension 0
There are 2 independent parts, one for each index of `parts`. A program takes and returns all parts, laid end to end along the dimension named above; each array names one. Nothing has to cross between parts.
Inputs may be any that keep to these rules, and one draw needn't show every extreme that they name: Every window_start is a multiple of 128 and at most 1024; some gene reaches 1024 in every draw. `gene_block`: a permutation of the genes. `cluster_sizes`: each row sums to 40.
All inputs are finite; a program needn't handle non-finite values.
Results may differ from a plain program's by a relative error of at most 0.0058.
Values may be sent and summed in bfloat16 or wider, within the bound.
A program may use at most 64 MiB of HBM per device.

v0:
```python
import jax
import jax.numpy as jnp
from jax import lax
from jax.sharding import PartitionSpec as P

W = 2048
SLOTS = 40
SPILL = 1024
ALIGN = 128


def shifted(block, axis, distance):
    devices = range(lax.axis_size(axis))
    route = [(i - distance, i) for i in devices if i - distance in devices]
    return lax.ppermute(block, axis, route)


def cluster_ratios(counts, cluster_sizes, valid_mask):
    cluster_ends = jnp.cumsum(cluster_sizes, axis=1, dtype=jnp.int32)
    slot_index = jnp.arange(SLOTS, dtype=jnp.int32)
    cluster_id = jnp.sum(
        (cluster_ends[:, None, :] <= slot_index[None, :, None]).astype(jnp.int32),
        axis=2,
        dtype=jnp.int32,
    )
    same_cluster = (cluster_id[:, :, None] == cluster_id[:, None, :]).astype(jnp.float32)
    live_counts = counts * valid_mask.astype(jnp.float32)[None, :, :]
    cluster_total = jnp.einsum(
        "sgj,gjk->sgk", live_counts, same_cluster, precision=lax.Precision.HIGHEST
    )
    return (live_counts / jnp.maximum(cluster_total, 1.0)).astype(jnp.bfloat16)


def tile_window(owner_block, offset, width):
    leading = owner_block.shape[:-1]
    tiles = owner_block.reshape(leading + (owner_block.shape[-1] // ALIGN, ALIGN))
    first_tile = offset // ALIGN
    piece = lax.dynamic_slice_in_dim(tiles, first_tile, width // ALIGN, len(leading))
    return piece.reshape(leading + (width,))


def window_slices(product, row_sum, row_square, starts, width):

    def window_of(owner_block, offset):
        return tile_window(owner_block, offset, width)

    cross_part = jax.vmap(window_of, in_axes=(0, 0))(product, starts)
    sum_part = jax.vmap(window_of, in_axes=(None, 0))(row_sum, starts)
    square_part = jax.vmap(window_of, in_axes=(None, 0))(row_square, starts)
    return (cross_part, sum_part, square_part)


def finish_stats(cross_part, sum_part, square_part, phen_sum, phen_square, sample_count):
    numerator = cross_part - sum_part[:, None, :] * phen_sum[:, :, None] / sample_count
    dose_var = jnp.maximum(square_part - sum_part * sum_part / sample_count, 1.0)
    pheno_var = jnp.maximum(phen_square - phen_sum * phen_sum / sample_count, 1.0)
    return (numerator * lax.rsqrt(dose_var)[:, None, :] * lax.rsqrt(pheno_var)[:, :, None]).astype(
        jnp.bfloat16
    )


def shards(dosage, expression, intron_counts, cluster_sizes, valid_mask, gene_block, window_start):
    samp_dev = dosage.shape[1]
    gene_dev = expression.shape[0]
    total_genes = gene_block.shape[0]
    next_rows = shifted(dosage[:SPILL], "genes", -1)
    dose_rows = jnp.concatenate([dosage, next_rows], axis=0)
    stored = intron_counts.reshape(intron_counts.shape[0], total_genes, SLOTS)
    counts = jnp.take(stored, gene_block, axis=1).astype(jnp.float32)
    ratios = cluster_ratios(counts, cluster_sizes, valid_mask).reshape(
        intron_counts.shape[0], total_genes * SLOTS
    )
    exchanged = lax.all_to_all(ratios, "genes", split_axis=1, concat_axis=0, tiled=True)
    intron_panel = exchanged.reshape(samp_dev, gene_dev, SLOTS)
    n_samples = lax.axis_size("samples")
    half_width = W // n_samples
    offset = lax.axis_index("samples") * half_width
    contract = (((0,), (1,)), ((), ()))
    expr_product = lax.dot_general(
        expression, dose_rows, (((1,), (1,)), ((), ())), preferred_element_type=jnp.float32
    )
    intron_product = lax.dot_general(
        exchanged, dose_rows, contract, preferred_element_type=jnp.float32
    )
    intron_product = intron_product.reshape(gene_dev, SLOTS, W + SPILL)
    product = jnp.concatenate([expr_product[:, None, :], intron_product], axis=1)
    expr_float = expression.astype(jnp.float32)
    intron_float = intron_panel.astype(jnp.float32)
    phen_sum = jnp.concatenate(
        [jnp.sum(expr_float, axis=1)[:, None], jnp.sum(intron_float, axis=0)], axis=1
    )
    phen_square = jnp.concatenate(
        [
            jnp.sum(expr_float * expr_float, axis=1)[:, None],
            jnp.sum(intron_float * intron_float, axis=0),
        ],
        axis=1,
    )
    dose_float = dose_rows.astype(jnp.float32)
    row_sum = jnp.sum(dose_float, axis=1)
    row_square = jnp.sum(dose_float * dose_float, axis=1)
    row_sum, row_square, phen_sum, phen_square = lax.psum(
        (row_sum, row_square, phen_sum, phen_square), "samples"
    )
    cross_part, sum_part, square_part = window_slices(product, row_sum, row_square, window_start, W)
    cross_sums = lax.psum_scatter(cross_part, "samples", scatter_dimension=2, tiled=True)
    sum_half = lax.dynamic_slice_in_dim(sum_part, offset, half_width, 1)
    square_half = lax.dynamic_slice_in_dim(square_part, offset, half_width, 1)
    sample_count = float(samp_dev * n_samples)
    return finish_stats(cross_sums, sum_half, square_half, phen_sum, phen_square, sample_count)


def solution(mesh):
    in_specs = (
        P(("parts", "genes"), "samples"),
        P(("parts", "genes"), "samples"),
        P(("parts", "samples", "genes"), None),
        P("parts", None),
        P("parts", None),
        P("parts"),
        P(("parts", "genes")),
    )
    out_specs = P(("parts", "genes"), None, "samples")
    return jax.shard_map(shards, mesh=mesh, in_specs=in_specs, out_specs=out_specs, check_vma=False)
```

profile of v0, /device:TPU:0, one launch (start us, length us, event | category | flops | bytes accessed | tf_op | source)
XLA Modules:
  0.0 140.2 jit_solution(9824551427102057853)
XLA Ops:
  6.5 3.2 %slice.3 = bf16[1024,1024]{1,0:T(8,128)(2,1)} slice(bf16[2048,1024]{1,0:T(8,128)(2,1)} %param.7), slice={[0:1024], [0:1024]} | slice | bytes 4194304 | tf_op jit(solution)/shard_map/slice | solution.py:66
  9.7 1.3 collective-permute-start
  11.7 0.7 gather_fusion
  12.4 3.1 %fusion.3 = bf16[128,64,40]{0,2,1:T(8,128)(2,1)} fusion(f32[64,40]{1,0:T(8,128)S(1)} %copy.35, bf16[64,128,40]{1,2,0:T(8,128)(2,1)S(1)} %gather_fusion, s32[64,40]{1,0:T(8,128)S(1)} %copy.36, pred[64]{0:T(512)(128)(4,1)S(1)} %compare_and_fusion), kind=kOutput, calls=%fused_computation.15 | convolution fusion | flops 160337920 | bytes 1331264 | tf_op jit(solution)/shard_map/sgj,gjk->sgk/dot_general | solution.py:28
  15.5 8.6 %all-to-all-start = ((bf16[128,8,320]{0,2,1:T(8,128)(2,1)}), bf16[128,8,320]{0,2,1:T(8,128)(2,1)S(1)}, u32[]{:S(2)}, u32[]{:S(2)}) async-start(bf16[128,8,320]{0,2,1:T(8,128)(2,1)} %bitcast.5), calls=%async_computation | async-start | bytes 1310720 | tf_op jit(solution)/shard_map/all_to_all | solution.py:73
  24.1 4.6 %constant_dynamic-update-slice_fusion.1 = bf16[3072,1024]{1,0:T(8,128)(2,1)} fusion(bf16[2048,1024]{1,0:T(8,128)(2,1)} %param.7), kind=kLoop, calls=%fused_computation.40 | loop fusion | bytes 8388608
  28.7 49.8 %all-to-all-done = bf16[128,8,320]{0,2,1:T(8,128)(2,1)S(1)} async-done(((bf16[128,8,320]{0,2,1:T(8,128)(2,1)}), bf16[128,8,320]{0,2,1:T(8,128)(2,1)S(1)}, u32[]{:S(2)}, u32[]{:S(2)}) %all-to-all-start) | async-done | bytes 655392 | tf_op jit(solution)/shard_map/all_to_all | solution.py:73
  78.6 1.5 %constant_dynamic-update-slice_fusion = bf16[3072,1024]{1,0:T(8,128)(2,1)} fusion(bf16[3072,1024]{1,0:T(8,128)(2,1)} %constant_dynamic-update-slice_fusion.1, bf16[1024,1024]{1,0:T(8,128)(2,1)S(1)} %collective-permute-done), kind=kLoop, calls=%fused_computation.39 | loop fusion | bytes 4194304 | tf_op jit(solution)/shard_map/concatenate | solution.py:67
  80.1 4.7 %convolution_bitcast_fusion = f32[8,1,24,128]{3,0,2,1:T(8,128)S(1)} fusion(bf16[3072,1024]{1,0:T(8,128)(2,1)} %constant_dynamic-update-slice_fusion, bf16[8,1024]{1,0:T(8,128)(2,1)S(1)} %copy-done.4), kind=kOutput, calls=%fused_computation.22 | convolution fusion | flops 50331648 | bytes 6406144 | tf_op jit(solution)/shard_map/dot_general | solution.py:79
  84.9 2.3 %fusion.18 = f32[8,40,24,128]{3,1,2,0:T(8,128)S(1)} fusion(bf16[8,40,1024,1]{2,1,3,0:T(8,128)(2,1)S(1)} %bitcast.75, bf16[24,128,1024,1]{2,1,0,3:T(8,128)(2,1)S(1)} %bitcast.73), kind=kOutput, calls=%fused_computation.55 | convolution fusion | flops 2013265920 | bytes 10878976 | tf_op jit(solution)/shard_map/dot_general | solution.py:82
  87.2 0.5 pad_maximum_fusion
  87.7 2.7 %copy.40 = f32[8,41,24,128]{3,1,0,2:T(8,128)} copy(f32[8,41,24,128]{3,1,2,0:T(8,128)S(1)} %pad_maximum_fusion) | data formatting | bytes 8060928 | tf_op jit(solution)/shard_map/concatenate | solution.py:86
  90.4 3.1 %gather_fusion.1 = f32[8,41,16,128]{3,1,2,0:T(8,128)S(1)} fusion(f32[8,41,24,128]{3,1,0,2:T(8,128)} %copy.40, s32[8]{0:T(128)S(1)} %or_bitcast_fusion), kind=kCustom, calls=%fused_computation.1 | custom fusion | bytes 5374080 | tf_op jit(solution)/shard_map/vmap()/gather | solution.py:38
  93.5 2.4 %copy.41 = f32[8,41,16,128]{3,2,0,1:T(8,128)} copy(f32[8,41,16,128]{3,1,2,0:T(8,128)S(1)} %gather_fusion.1) | data formatting | bytes 5373952 | tf_op jit(solution)/shard_map/vmap()/gather | solution.py:38
  95.9 3.9 %reshape.50 = f32[8,41,2048]{2,0,1:T(8,128)} reshape(f32[8,41,16,128]{3,2,0,1:T(8,128)} %copy.41) | data formatting | bytes 5373952 | tf_op jit(solution)/shard_map/vmap()/reshape | solution.py:39
  100.2 0.7 copy-done.2
  101.4 5.5 %convert_reduce_fusion = (f32[3072]{0:T(1024)S(1)}, f32[3072]{0:T(1024)S(1)}) fusion(bf16[3072,1024]{1,0:T(8,128)(2,1)} %constant_dynamic-update-slice_fusion), kind=kLoop, calls=%fused_computation.7 | loop fusion | flops 12576768 | bytes 6316032 | tf_op jit(solution)/shard_map/reduce_sum | solution.py:100
  106.9 3.4 %all-reduce.1 = (f32[8,41]{1,0:T(8,128)S(1)}, f32[8,41]{1,0:T(8,128)S(1)}, f32[24,128]{1,0:T(8,128)S(1)}, f32[24,128]{1,0:T(8,128)S(1)}) all-reduce(f32[8,41]{1,0:T(8,128)S(1)} %get-tuple-element.50, f32[8,41]{1,0:T(8,128)S(1)} %get-tuple-element.49, ...), channel_id=1, replica_groups=mesh['parts'=2,'genes'=8,'samples'=2] {'samples'}, use_global_device_ids=true, to_apply=%region_12.13 | all-reduce | flops 6800 | bytes 54400 | tf_op jit(solution)/shard_map/psum | solution.py:102
  110.3 10.1 %while.3 = (s32[]{:T(128)}, f32[24,128]{1,0:T(8,128)S(1)}, s32[8,2]{0,1:T(2,128)S(1)}, f32[8,16,128]{2,1,0:T(8,128)S(1)}, s32[]{:T(128)}) while((s32[]{:T(128)}, f32[24,128]{1,0:T(8,128)S(1)}, s32[8,2]{0,1:T(2,128)S(1)}, f32[8,16,128]{2,1,0:T(8,128)S(1)}, s32[]{:T(128)}) %tuple.35), condition=%wide.while_cond.1, body=%wide.while_body.1.sunk | while | flops 2 | bytes 16481 | solution.py:38
  110.4 0.5 slice.35
  110.9 0.7 bitcast_dynamic-update-slice_fusion.5
  111.7 0.5 slice.35
  112.2 0.7 bitcast_dynamic-update-slice_fusion.5
  112.9 0.5 slice.35
  113.4 0.7 bitcast_dynamic-update-slice_fusion.5
  114.2 0.5 slice.35
  114.7 0.7 bitcast_dynamic-update-slice_fusion.5
  115.5 0.5 slice.35
  116.0 0.7 bitcast_dynamic-update-slice_fusion.5
  117.2 0.7 bitcast_dynamic-update-slice_fusion.5
  118.0 0.5 slice.35
  118.5 0.7 bitcast_dynamic-update-slice_fusion.5
  119.3 0.5 slice.35
  119.8 0.7 bitcast_dynamic-update-slice_fusion.5
  120.5 10.1 %while.2 = (s32[]{:T(128)}, f32[24,128]{1,0:T(8,128)S(1)}, s32[8,2]{0,1:T(2,128)S(1)}, f32[8,16,128]{2,1,0:T(8,128)S(1)}, s32[]{:T(128)}) while((s32[]{:T(128)}, f32[24,128]{1,0:T(8,128)S(1)}, s32[8,2]{0,1:T(2,128)S(1)}, f32[8,16,128]{2,1,0:T(8,128)S(1)}, s32[]{:T(128)}) %tuple.40), condition=%wide.while_cond, body=%wide.while_body.sunk | while | flops 2 | bytes 16481 | solution.py:38
  120.6 0.5 slice.34
  121.1 0.7 bitcast_dynamic-update-slice_fusion.4
  121.8 0.5 slice.34
  122.4 0.7 bitcast_dynamic-update-slice_fusion.4
  123.1 0.5 slice.34
  123.6 0.7 bitcast_dynamic-update-slice_fusion.4
  124.4 0.5 slice.34
  124.9 0.7 bitcast_dynamic-update-slice_fusion.4
  126.1 0.7 bitcast_dynamic-update-slice_fusion.4
  127.4 0.7 bitcast_dynamic-update-slice_fusion.4
  128.7 0.7 bitcast_dynamic-update-slice_fusion.4
  129.9 0.7 bitcast_dynamic-update-slice_fusion.4
  130.9 2.5 %multiply_convert_fusion = bf16[8,41,1024]{2,0,1:T(8,128)(2,1)} fusion(f32[8,41,1024]{2,0,1:T(8,128)} %reduce-scatter.2.cloned.1.call-done, f32[8,41]{0,1:T(8,128)S(1)} %copy.45, f32[8,1024]{1,0:T(8,128)S(1)} %get-tuple-element.48, f32[8,41]{0,1:T(8,128)S(1)} %copy.43, f32[8,1024]{1,0:T(8,128)S(1)} %get-tuple-element.47), kind=kLoop, calls=%fused_computation.16 | loop fusion | flops 2015232 | bytes 2083392 | tf_op jit(solution)/shard_map/convert_element_type | solution.py:57
  (71 shorter events, 5.8 us)
Async XLA Ops:
  6.5 4.5 %copy-start.7 = (s32[64]{0:T(128)S(1)}, s32[64]{0:T(128)}, u32[]{:S(2)}) copy-start(s32[64]{0:T(128)} %param.12) | copy-start | bytes 772
  6.5 4.5 %copy-start.6 = (s32[64,8]{0,1:T(8,128)S(1)}, s32[64,8]{0,1:T(8,128)}, u32[]{:S(2)}) copy-start(s32[64,8]{0,1:T(8,128)} %param.10) | copy-start | bytes 6148
  6.5 4.6 %copy-start.3 = (bf16[128,2560]{1,0:T(8,128)(2,1)S(1)}, bf16[128,2560]{1,0:T(8,128)(2,1)}, u32[]{:S(2)}) copy-start(bf16[128,2560]{1,0:T(8,128)(2,1)} %param.9) | copy-start | bytes 1966084
  6.5 5.0 %copy-start.5 = (s32[64,40]{0,1:T(8,128)S(1)}, s32[64,40]{0,1:T(8,128)}, u32[]{:S(2)}) copy-start(s32[64,40]{0,1:T(8,128)} %param.11) | copy-start | bytes 30724
  9.7 68.9 %collective-permute-start = (bf16[1024,1024]{1,0:T(8,128)(2,1)}, bf16[1024,1024]{1,0:T(8,128)(2,1)S(1)}, u32[]{:S(2)}, u32[]{:S(2)}) collective-permute-start(bf16[1024,1024]{1,0:T(8,128)(2,1)} %slice.3), channel_id=1, source_target_pairs={{2,0},{4,2},{6,4},{8,6},{10,8},{12,10},{14,12},{3,1},{5,3},{7,5},{... | collective-permute-start | bytes 6291464 | tf_op jit(solution)/shard_map/ppermute | solution.py:15
  12.4 11.7 %copy-start.8 = (s32[8]{0:T(128)S(1)}, s32[8]{0:T(128)}, u32[]{:S(2)}) copy-start(s32[8]{0:T(128)} %param.13) | copy-start | bytes 100
  15.5 63.0 %all-to-all-start = ((bf16[128,8,320]{0,2,1:T(8,128)(2,1)}), bf16[128,8,320]{0,2,1:T(8,128)(2,1)S(1)}, u32[]{:S(2)}, u32[]{:S(2)}) async-start(bf16[128,8,320]{0,2,1:T(8,128)(2,1)} %bitcast.5), calls=%async_computation | async-start | bytes 1310720 | tf_op jit(solution)/shard_map/all_to_all | solution.py:73
  24.0 106.9 %reduce-scatter.2.cloned.1.call-start = ((), (), s32[]{:S(2)}) async-start(), calls=%async_computation.2 | async-start | bytes 4030464 | tf_op jit(solution)/shard_map/reduce_scatter | solution.py:106
  28.7 51.4 %copy-start.4 = (bf16[8,1024]{1,0:T(8,128)(2,1)S(1)}, bf16[8,1024]{1,0:T(8,128)(2,1)}, u32[]{:S(2)}) copy-start(bf16[8,1024]{1,0:T(8,128)(2,1)} %param.8) | copy-start | bytes 49156
  78.5 1.6 %copy-start.1 = (bf16[128,8,320]{0,2,1:T(8,128)(2,1)}, bf16[128,8,320]{0,2,1:T(8,128)(2,1)S(1)}, u32[]{:S(2)}) copy-start(bf16[128,8,320]{0,2,1:T(8,128)(2,1)S(1)} %all-to-all-done) | copy-start | bytes 1966084
  80.1 4.8 %copy-start = (bf16[3072,1024]{1,0:T(8,128)(2,1)S(1)}, bf16[3072,1024]{1,0:T(8,128)(2,1)}, u32[]{:S(2)}) copy-start(bf16[3072,1024]{1,0:T(8,128)(2,1)} %constant_dynamic-update-slice_fusion) | copy-start | bytes 18874372
  99.8 1.1 copy-start.2
Sparse Core Ops, SparseCore 0:
  99.9 7.5 reduce-scatter.1
where the time goes:
time: 141 us; the launch traced here: 140 us
  waiting for transfers between devices  49.8 us (35%)
  local copies, waits for them, and re-layouts  43.9 us (31%)
  between operations  13.7 us (10%)
  matrix products  10 us (7%)
  starting transfers between devices  9.88 us (7%)
  other arithmetic  9.15 us (6%)
  blocking collectives  3.42 us (2%)
    all_to_all x1, waiting for transfers between devices, shards(): lax.all_to_all(ratios, 'genes', split_axis=1, concat_axis=0, tiled=True)  49.8 us
    gather x48, local copies, waits for them, and re-layouts  19.9 us
    all_to_all x1, starting transfers between devices, shards(): lax.all_to_all(ratios, 'genes', split_axis=1, concat_axis=0, tiled=True)  8.56 us
    unnamed x24, local copies, waits for them, and re-layouts  5.68 us
    reduce_sum x1, other arithmetic, shards(): row_sum = jnp.sum(dose_float, axis=1)  5.48 us
    gather x2, local copies, waits for them, and re-layouts, tile_window(): lax.dynamic_slice_in_dim(tiles, first_tile, width // ALIGN, len(leading))  5.48 us
    dot_general x1, matrix products, shards(): lax.dot_general(expression, dose_rows, (((1,), (1,)), ((), ())), preferre...  4.66 us
    reshape x1, local copies, waits for them, and re-layouts, tile_window(): return piece.reshape(leading + (width,))  3.89 us
  transfers between devices with their start and end apart: 3, of which 1 were waited for; matrix products, arithmetic and copies ran while one was open for 25% of the time, Pallas kernels for 0%

commit v1 on v0

v1 whole, which is shorter than its diff:
```python
import functools

import jax
import jax.numpy as jnp
from jax import lax
from jax.experimental import pallas as pl
from jax.experimental.pallas import tpu as pltpu
from jax.sharding import PartitionSpec as P

LANE = 128
SPILL = 1024
MESH = pl.DeviceIdType.MESH


def lane_tiles_sum(value):
    total = value[:, :LANE]
    for t in range(1, value.shape[1] // LANE):
        total = total + value[:, t * LANE : (t + 1) * LANE]
    return total


def kernel(
    n, genes, slots, starts_ref, block_ref, counts_ref, mix_ref, expr_ref, dose_hbm, out_ref,
    dose, stage, sendbuf, recv, halo, halo_expr, pheno, hpheno, prod, hprod, hprod_in,
    sel_out, sel_in, own_res, halo_full, dstat, dstat_in, pstat, pstat_in, hstat, hstat_in,
    hres, hres_in, win, dose_sem, a2a_send, a2a_recv, fwd_send, fwd_recv, pair_send, pair_recv,
    back_send, back_recv,
):
    me = lax.axis_index("genes")
    core = lax.axis_index("samples")
    other = 1 - core
    rows, samp = dose.shape
    phen = slots + 1
    width = rows // 2
    half = SPILL // 2
    intron_rows = slots * genes
    all_rows = phen * genes
    blk = counts_ref.shape[2]
    count = float(2 * samp)
    shift = n // 2

    dose_copy = pltpu.make_async_copy(dose_hbm, dose, dose_sem)
    dose_copy.start()

    barrier = pltpu.get_barrier_semaphore()

    def greet(k, carry):
        there = lax.rem(me + k, n)
        pl.semaphore_signal(
            barrier, inc=1, device_id={"genes": there, "samples": core}, device_id_type=MESH
        )
        pl.semaphore_signal(
            barrier, inc=1, device_id={"genes": there, "samples": other}, device_id_type=MESH
        )
        return carry

    lax.fori_loop(1, n, greet, 0)
    pl.semaphore_signal(barrier, inc=1, device_id={"samples": other}, device_id_type=MESH)

    def a2a(owner, source):
        return pltpu.make_async_remote_copy(
            src_ref=sendbuf.at[owner], dst_ref=recv.at[source],
            send_sem=a2a_send.at[owner], recv_sem=a2a_recv.at[source],
            device_id={"genes": owner}, device_id_type=MESH,
        )

    def make_block(owner):
        for g in range(genes):
            gene = owner * genes + g
            cnt = counts_ref[block_ref[gene]].astype(jnp.bfloat16)
            both = jnp.dot(mix_ref[gene], cnt, preferred_element_type=jnp.float32)
            ratio = both[slots:] / jnp.maximum(both[:slots], 1.0)
            stage[pl.ds(g, slots, stride=genes), :] = ratio
        sendbuf[owner] = stage[...].astype(jnp.bfloat16)

    make_block(lax.rem(me + shift, n))
    pl.semaphore_wait(barrier, 2 * n - 1)

    def ratio_step(k, carry):
        make_block(lax.rem(me + shift + k, n))

        @pl.when(k - 1 != n - shift)
        def _():
            a2a(lax.rem(me + shift + k - 1, n), me).start()

        return carry

    lax.fori_loop(1, n, ratio_step, 0)
    a2a(lax.rem(me + shift + n - 1, n), me).start()

    dose_copy.wait()
    dstat[:, rows:] = jnp.zeros((16, SPILL), jnp.float32)
    ones = jnp.ones((8, LANE), jnp.float32)
    chunk = 256

    def dose_stat(k, carry):
        at = pl.multiple_of(k * chunk, chunk)
        value = dose[pl.ds(at, chunk), :].astype(jnp.float32)
        dims = (((1,), (1,)), ((), ()))
        for slot, part in ((0, value), (8, value * value)):
            dstat[slot : slot + 8, pl.ds(at, chunk)] = lax.dot_general(
                ones, lane_tiles_sum(part), dims, precision=lax.Precision.HIGHEST,
                preferred_element_type=jnp.float32,
            )
        return carry

    lax.fori_loop(0, rows // chunk, dose_stat, 0)

    def pair(k, src, dst):
        return pltpu.make_async_remote_copy(
            src_ref=src, dst_ref=dst, send_sem=pair_send.at[k], recv_sem=pair_recv.at[k],
            device_id={"samples": other}, device_id_type=MESH,
        )

    def fwd(src, dst, k):
        return pltpu.make_async_remote_copy(
            src_ref=src, dst_ref=dst, send_sem=fwd_send.at[k], recv_sem=fwd_recv.at[k],
            device_id={"genes": lax.rem(me + 1, n)}, device_id_type=MESH,
        )

    has_next = me < n - 1
    has_prev = me > 0

    @pl.when(has_next)
    def _():
        fwd(expr_ref, halo_expr, n).start()
        fwd(sendbuf.at[me], halo.at[me], me).start()

    def relay(k, carry):
        source = lax.rem(me + 2 * n - shift - k, n)

        @pl.when(k != n - shift)
        def _():
            a2a(source, source).wait_recv()

            @pl.when(has_next)
            def _():
                fwd(recv.at[source], halo.at[source], source).start()

        return carry

    dstat_pair = pair(0, dstat, dstat_in)
    dstat_pair.start()
    lax.fori_loop(0, n, relay, 0)
    recv[me] = sendbuf[me]

    def pack(blocks, expr_rows, target, stat):
        for i in range(n):
            target[:intron_rows, i * blk : (i + 1) * blk] = blocks[i]
        target[intron_rows:, :] = expr_rows[...]
        value = target[...].astype(jnp.float32)
        stat[0] = lane_tiles_sum(value)
        stat[1] = lane_tiles_sum(value * value)

    pack(recv, expr_ref, pheno, pstat)
    pstat_pair = pair(1, pstat, pstat_in)

    dims = (((1,), (1,)), ((), ()))
    prod[:, rows:] = jnp.zeros((all_rows, SPILL), jnp.float32)

    def own_dot(k, carry):
        at = pl.multiple_of(k * chunk, chunk)
        prod[:, pl.ds(at, chunk)] = lax.dot_general(
            pheno[...], dose[pl.ds(at, chunk), :], dims, preferred_element_type=jnp.float32
        )
        return carry

    lax.fori_loop(0, rows // chunk, own_dot, 0)
    pstat_pair.start()

    lane_gene = lax.broadcasted_iota(jnp.int32, (genes, LANE), 0)
    starts = jnp.zeros((genes, LANE), jnp.int32)
    for g in range(genes):
        starts = jnp.where(lane_gene == g, starts_ref[g], starts)
    steps = SPILL // LANE
    at_step = [starts == s * LANE for s in range(steps)]

    def windows(source, row, base):
        tiles = []
        for t in range((width + SPILL) // LANE):
            at = pl.multiple_of(base + t * LANE, LANE)
            tiles.append(source[pl.ds(row, genes), pl.ds(at, LANE)])
        picked = []
        for t in range(width // LANE):
            tile = tiles[t + steps]
            for s in range(steps):
                tile = jnp.where(at_step[s], tiles[t + s], tile)
            picked.append(tile)
        return picked

    def select_out(p, carry):
        row = pl.multiple_of(p * genes, genes)
        for t, tile in enumerate(windows(prod, row, other * width)):
            sel_out[pl.ds(row, genes), t * LANE : (t + 1) * LANE] = tile
        return carry

    lax.fori_loop(0, phen, select_out, 0)
    sel_pair = pair(2, sel_out, sel_in)
    sel_pair.start()

    dstat_pair.wait_recv()
    dstat_pair.wait_send()
    dstat[...] = dstat[...] + dstat_in[...]

    def scales(stat, stat_in, row):
        total = jnp.sum(stat[0, pl.ds(row, genes), :] + stat_in[0, pl.ds(row, genes), :], axis=1, keepdims=True)
        square = jnp.sum(stat[1, pl.ds(row, genes), :] + stat_in[1, pl.ds(row, genes), :], axis=1, keepdims=True)
        return total / count, lax.rsqrt(jnp.maximum(square - total * total / count, 1.0))

    def dose_scale(total, square):
        return lax.rsqrt(jnp.maximum(square - total * total / count, 1.0))

    hstat_pair = pair(3, hstat, hstat_in)
    hprod_pair = pair(4, hprod.at[other], hprod_in)
    back = pltpu.make_async_remote_copy(
        src_ref=hres, dst_ref=hres_in.at[core], send_sem=back_send, recv_sem=back_recv.at[core],
        device_id={"genes": lax.rem(me + n - 1, n), "samples": 1}, device_id_type=MESH,
    )

    @pl.when(has_prev)
    def _():
        fwd(expr_ref, halo_expr, n).wait_recv()

        def arrive(k, carry):
            fwd(recv.at[k], halo.at[k], k).wait_recv()
            return carry

        lax.fori_loop(0, n, arrive, 0)
        pack(halo, halo_expr, hpheno, hstat)

        def halo_dot(k, carry):
            at = pl.multiple_of(k * half, half)
            hprod[k] = lax.dot_general(
                hpheno[...], dose[pl.ds(at, half), :], dims, preferred_element_type=jnp.float32
            )
            return carry

        lax.fori_loop(0, 2, halo_dot, 0)
        hstat_pair.start()
        hprod_pair.start()

    pstat_pair.wait_recv()
    sel_pair.wait_recv()
    win_sum = windows(dstat, 0, core * width)
    win_square = windows(dstat, 8, core * width)
    for t in range(width // LANE):
        cols = slice(t * LANE, (t + 1) * LANE)
        win[0:8, cols] = win_sum[t]
        win[8:16, cols] = dose_scale(win_sum[t], win_square[t])

    @pl.when(has_prev)
    def _():
        hstat_pair.wait_recv()
        hprod_pair.wait_recv()
        at = pl.multiple_of(core * half, half)
        sums = dstat[0:8, pl.ds(at, half)]
        scale = dose_scale(sums, dstat[8:16, pl.ds(at, half)])

        def halo_out(p, carry):
            row = pl.multiple_of(p * genes, genes)
            mean, inv = scales(hstat, hstat_in, row)
            cross = hprod[core, pl.ds(row, genes), :] + hprod_in[pl.ds(row, genes), :]
            hres[p] = ((cross - sums * mean) * scale * inv).astype(jnp.bfloat16)
            return carry

        lax.fori_loop(0, phen, halo_out, 0)
        back.start()

    def own_out(p, carry):
        row = pl.multiple_of(p * genes, genes)
        mean, inv = scales(pstat, pstat_in, row)
        for t, tile in enumerate(windows(prod, row, core * width)):
            cols = slice(t * LANE, (t + 1) * LANE)
            cross = tile + sel_in[pl.ds(row, genes), cols]
            own_res[pl.ds(row, genes), cols] = (cross - win[0:8, cols] * mean) * win[8:16, cols] * inv
        return carry

    lax.fori_loop(0, phen, own_out, 0)
    takes_halo = jnp.logical_and(has_next, core == 1)

    @pl.when(takes_halo)
    def _():
        for side in range(2):
            pltpu.make_async_remote_copy(
                src_ref=hres, dst_ref=hres_in.at[side], send_sem=back_send,
                recv_sem=back_recv.at[side],
                device_id={"genes": lax.rem(me + n - 1, n), "samples": 1}, device_id_type=MESH,
            ).wait_recv()
        halo_full[:, :width] = jnp.zeros((all_rows, width), jnp.float32)

        def widen(p, carry):
            row = pl.multiple_of(p * genes, genes)
            for side in range(2):
                halo_full[pl.ds(row, genes), width + side * half : width + (side + 1) * half] = (
                    hres_in[side, p].astype(jnp.float32)
                )
            return carry

        lax.fori_loop(0, phen, widen, 0)

        def add_halo(p, carry):
            row = pl.multiple_of(p * genes, genes)
            for t, tile in enumerate(windows(halo_full, row, 0)):
                cols = slice(t * LANE, (t + 1) * LANE)
                out_ref[lax.rem(p + 1, phen), :, cols] = (
                    own_res[pl.ds(row, genes), cols] + tile
                ).astype(jnp.bfloat16)
            return carry

        lax.fori_loop(0, phen, add_halo, 0)

    @pl.when(jnp.logical_not(takes_halo))
    def _():
        def plain(p, carry):
            row = pl.multiple_of(p * genes, genes)
            out_ref[lax.rem(p + 1, phen)] = own_res[pl.ds(row, genes), :].astype(jnp.bfloat16)
            return carry

        lax.fori_loop(0, phen, plain, 0)

    def drain(k, carry):
        a2a(lax.rem(me + k, n), me).wait_send()
        return carry

    lax.fori_loop(1, n, drain, 0)
    pstat_pair.wait_send()
    sel_pair.wait_send()

    @pl.when(has_next)
    def _():
        fwd(expr_ref, halo_expr, n).wait_send()

        def drain_fwd(k, carry):
            fwd(recv.at[k], halo.at[k], k).wait_send()
            return carry

        lax.fori_loop(0, n, drain_fwd, 0)

    @pl.when(has_prev)
    def _():
        hstat_pair.wait_send()
        hprod_pair.wait_send()
        back.wait_send()


def mixing(cluster_sizes, valid_mask):
    slots = valid_mask.shape[1]
    clusters = cluster_sizes.shape[1]
    slot = jnp.arange(slots, dtype=jnp.int32)
    ends = []
    for c in range(clusters):
        ends.append(cluster_sizes[:, c] + (ends[-1] if c else 0))
    cluster_id = sum((end[:, None] <= slot[None, :]).astype(jnp.int32) for end in ends)
    same = cluster_id[:, :, None] == cluster_id[:, None, :]
    diag = jnp.broadcast_to((slot[:, None] == slot[None, :])[None], same.shape)
    both = jnp.concatenate([same, diag], axis=1)
    return jnp.where(both, valid_mask[:, None, :], 0).astype(jnp.bfloat16)


def shards(dosage, expression, intron_counts, cluster_sizes, valid_mask, gene_block, window_start):
    n = lax.axis_size("genes")
    rows, samp = dosage.shape
    genes = expression.shape[0]
    slots = valid_mask.shape[1]
    blk = intron_counts.shape[0]
    phen = slots + 1
    all_rows = phen * genes
    width = rows // 2
    half = SPILL // 2
    counts_t = intron_counts.T.astype(jnp.float32).reshape(n * genes, slots, blk)
    mix = mixing(cluster_sizes, valid_mask)
    vmem = pl.BlockSpec(memory_space=pltpu.VMEM)
    smem = pl.BlockSpec(memory_space=pltpu.SMEM)
    f32, bf16 = jnp.float32, jnp.bfloat16
    dma = pltpu.SemaphoreType.DMA
    result = pl.pallas_call(
        functools.partial(kernel, n, genes, slots),
        out_shape=jax.ShapeDtypeStruct((phen, genes, width), bf16),
        in_specs=[smem, smem, vmem, vmem, vmem, pl.BlockSpec(memory_space=pl.ANY)],
        out_specs=vmem,
        scratch_shapes=[
            pltpu.VMEM((rows, samp), bf16),
            pltpu.VMEM((slots * genes, blk), f32),
            pltpu.VMEM((n, slots * genes, blk), bf16),
            pltpu.VMEM((n, slots * genes, blk), bf16),
            pltpu.VMEM((n, slots * genes, blk), bf16),
            pltpu.VMEM((genes, samp), bf16),
            pltpu.VMEM((all_rows, samp), bf16),
            pltpu.VMEM((all_rows, samp), bf16),
            pltpu.VMEM((all_rows, rows + SPILL), f32),
            pltpu.VMEM((2, all_rows, half), f32),
            pltpu.VMEM((all_rows, half), f32),
            pltpu.VMEM((all_rows, width), f32),
            pltpu.VMEM((all_rows, width), f32),
            pltpu.VMEM((all_rows, width), f32),
            pltpu.VMEM((all_rows, width + SPILL), f32),
            pltpu.VMEM((16, rows + SPILL), f32),
            pltpu.VMEM((16, rows + SPILL), f32),
            pltpu.VMEM((2, all_rows, LANE), f32),
            pltpu.VMEM((2, all_rows, LANE), f32),
            pltpu.VMEM((2, all_rows, LANE), f32),
            pltpu.VMEM((2, all_rows, LANE), f32),
            pltpu.VMEM((phen, genes, half), bf16),
            pltpu.VMEM((2, phen, genes, half), bf16),
            pltpu.VMEM((16, width), f32),
            dma, dma((n,)), dma((n,)), dma((n + 1,)), dma((n + 1,)), dma((5,)), dma((5,)),
            dma, dma((2,)),
        ],
        compiler_params=pltpu.CompilerParams(
            collective_id=0, has_side_effects=True, vmem_limit_bytes=62 * 1024 * 1024
        ),
    )(window_start, gene_block, counts_t, mix, expression, dosage)
    return jnp.transpose(result, (1, 0, 2))


def solution(mesh):
    in_specs = (
        P(("parts", "genes"), "samples"),
        P(("parts", "genes"), "samples"),
        P(("parts", "samples", "genes"), None),
        P("parts", None),
        P("parts", None),
        P("parts"),
        P(("parts", "genes")),
    )
    out_specs = P(("parts", "genes"), None, "samples")
    return jax.shard_map(shards, mesh=mesh, in_specs=in_specs, out_specs=out_specs, check_vma=False)
```

time: 141 us -> 62.6 us (0.44)
  the two profiles are of different devices: /device:TPU:0 before, /device:TPU:15 now
where the time goes in v1:
time: 62.6 us; the launch traced here: 62.3 us
  Pallas kernels  55.2 us (88%)
  local copies, waits for them, and re-layouts  3.62 us (6%)
  other arithmetic  3.44 us (5%)
    pallas_call x1, Pallas kernels, shards(): pl.pallas_call(functools.partial(kernel, n, genes, slots), out_shape=jax....  55.2 us
    unnamed x6, local copies, waits for them, and re-layouts  2.07 us
    convert_element_type x1, other arithmetic, mixing(): return jnp.where(both, valid_mask[:, None, :], 0).astype(jnp.bfloat16)  1.55 us
    reshape x1, local copies, waits for them, and re-layouts, shards(): intron_counts.T.astype(jnp.float32).reshape(n * genes, slots, blk)  1.46 us

profile of v1, /device:TPU:15, one launch (start us, length us, event | category | flops | bytes accessed | tf_op | source)
XLA Modules:
  0.0 62.3 jit_solution(6698620929487021704)
XLA Ops:
  0.0 1.2 %convert_bitcast_fusion = f32[2560,128]{0,1:T(8,128)S(1)} fusion(bf16[128,2560]{1,0:T(8,128)(2,1)} %param.9), kind=kLoop, calls=%fused_computation.1 | loop fusion | flops 327680 | bytes 1966080 | tf_op jit(solution)/shard_map/reshape | solution.py:370
  1.2 0.0 copy-start.1
  1.2 0.0 copy-start
  1.2 1.5 %copy.8 = f32[2560,128]{1,0:T(8,128)} copy(f32[2560,128]{0,1:T(8,128)S(1)} %convert_bitcast_fusion) | data formatting | bytes 2621440 | tf_op jit(solution)/shard_map/reshape | solution.py:370
  2.7 0.1 broadcast_in_dim.10
  2.8 0.0 copy-done.1
  2.9 0.1 convert_add_fusion
  3.0 0.5 broadcast_compare_fusion
  3.5 0.0 copy-done
  3.5 0.1 copy.9
  3.6 1.5 %select_convert_fusion.mix_ref = bf16[64,80,40]{2,1,0:T(8,128)(2,1)} fusion(pred[64,40,40]{2,1,0:T(8,128)(4,1)S(1)} %broadcast_in_dim.10, pred[64,40,40]{2,1,0:T(8,128)(4,1)S(1)} %broadcast_compare_fusion, s32[64,40]{1,0:T(8,128)S(1)} %copy.9), kind=kLoop, calls=%fused_computation | loop fusion | flops 614400 | bytes 624640 | tf_op jit(solution)/shard_map/convert_element_type | solution.py:357
  5.2 55.2 %shard_map.73 = bf16[41,8,1024]{2,1,0:T(8,128)(2,1)} custom-call(s32[8]{0:T(128)} %starts_ref.1, s32[64]{0:T(128)} %block_ref.1, f32[64,40,128]{2,1,0:T(8,128)} %bitcast.18, bf16[64,80,40]{2,1,0:T(8,128)(2,1)} %select_convert_fusion.mix_ref, bf16[8,1024]{1,0:T(8,128)(2,1)} %expr_ref.1, bf16[2048,1024]{1,0:T(8,128)(2,1)} %dose_hbm.1), custom_call_target="tpu_custom_call" | custom-call | tf_op jit(solution)/shard_map/pallas_call | solution.py:376
  60.4 2.0 %copy.11 = bf16[8,41,1024]{2,0,1:T(8,128)(2,1)} copy(bf16[8,41,1024]{2,0,1:T(8,128)(2,1)} %bitcast.19) | data formatting | bytes 1343488
  (4 shorter events, 0.0 us)
Async XLA Ops:
  1.2 1.6 %copy-start.1 = (s32[64,8]{0,1:T(8,128)S(1)}, s32[64,8]{0,1:T(8,128)}, u32[]{:S(2)}) copy-start(s32[64,8]{0,1:T(8,128)} %param.10) | copy-start | bytes 6148
  1.2 2.3 %copy-start = (s32[64,40]{0,1:T(8,128)S(1)}, s32[64,40]{0,1:T(8,128)}, u32[]{:S(2)}) copy-start(s32[64,40]{0,1:T(8,128)} %param.11) | copy-start | bytes 30724

commit v2 on v1

--- a/solution.py
+++ b/solution.py
@@ -20,11 +20,11 @@
 
 
 def kernel(
-    n, genes, slots, starts_ref, block_ref, counts_ref, mix_ref, expr_ref, dose_hbm, out_ref,
-    dose, stage, sendbuf, recv, halo, halo_expr, pheno, hpheno, prod, hprod, hprod_in,
+    n, genes, slots, starts_ref, block_ref, counts_ref, sizes_ref, valid_ref, expr_ref, dose_hbm, out_ref,
+    dose, ids, stage, sendbuf, recv, halo, halo_expr, pheno, hpheno, prod, hprod, hprod_in,
     sel_out, sel_in, own_res, halo_full, dstat, dstat_in, pstat, pstat_in, hstat, hstat_in,
     hres, hres_in, win, dose_sem, a2a_send, a2a_recv, fwd_send, fwd_recv, pair_send, pair_recv,
-    back_send, back_recv,
+    back_send, back_recv, ext_send,
 ):
     me = lax.axis_index("genes")
     core = lax.axis_index("samples")
@@ -64,29 +64,73 @@
             device_id={"genes": owner}, device_id_type=MESH,
         )
 
+    slot_at = lax.broadcasted_iota(jnp.int32, ids.shape, 1)
+    end = jnp.zeros((ids.shape[0], 1), jnp.int32)
+    cluster_of = jnp.zeros(ids.shape, jnp.int32)
+    for c in range(sizes_ref.shape[1]):
+        end = end + sizes_ref[:, c : c + 1]
+        cluster_of = cluster_of + (end <= slot_at).astype(jnp.int32)
+    ids[...] = cluster_of
+    clusters = sizes_ref.shape[1]
+    cluster_row = lax.broadcasted_iota(jnp.int32, (clusters, slots), 0)
+    on_diagonal = lax.broadcasted_iota(jnp.int32, (slots, slots), 0) == lax.broadcasted_iota(
+        jnp.int32, (slots, slots), 1
+    )
+
     def make_block(owner):
         for g in range(genes):
             gene = owner * genes + g
-            cnt = counts_ref[block_ref[gene]].astype(jnp.bfloat16)
-            both = jnp.dot(mix_ref[gene], cnt, preferred_element_type=jnp.float32)
-            ratio = both[slots:] / jnp.maximum(both[:slots], 1.0)
+            cnt = counts_ref[block_ref[gene]]
+            valid = valid_ref[pl.ds(gene, 1), :].astype(jnp.float32)
+            member = (cluster_row == ids[pl.ds(gene, 1), :]).astype(jnp.float32)
+            same = lax.dot_general(
+                member.astype(jnp.bfloat16), (member * valid).astype(jnp.bfloat16),
+                (((0,), (0,)), ((), ())), preferred_element_type=jnp.float32,
+            ).astype(jnp.bfloat16)
+            keep = jnp.where(on_diagonal, valid, 0.0).astype(jnp.bfloat16)
+            total = jnp.dot(same, cnt, preferred_element_type=jnp.float32)
+            live = jnp.dot(keep, cnt, preferred_element_type=jnp.float32)
+            ratio = live / jnp.maximum(total, 1.0)
             stage[pl.ds(g, slots, stride=genes), :] = ratio
         sendbuf[owner] = stage[...].astype(jnp.bfloat16)
 
+    def side(index):
+        return index * 2 // n
+
+    def relayed(source, owner):
+        return jnp.logical_and(side(source) != side(owner), side(owner) == side(owner + 1))
+
+    def ext(owner):
+        return pltpu.make_async_remote_copy(
+            src_ref=sendbuf.at[owner], dst_ref=halo.at[me],
+            send_sem=ext_send.at[owner], recv_sem=fwd_recv.at[me],
+            device_id={"genes": lax.rem(owner + 1, n)}, device_id_type=MESH,
+        )
+
+    def extends(owner):
+        far = jnp.logical_and(owner != n - 1, owner + 1 != me)
+        return jnp.logical_and(far, jnp.logical_not(relayed(me, owner)))
+
+    def send_block(owner):
+        @pl.when(owner != me)
+        def _():
+            a2a(owner, me).start()
+
+        @pl.when(extends(owner))
+        def _():
+            ext(owner).start()
+
     make_block(lax.rem(me + shift, n))
     pl.semaphore_wait(barrier, 2 * n - 1)
 
     def ratio_step(k, carry):
         make_block(lax.rem(me + shift + k, n))
 
-        @pl.when(k - 1 != n - shift)
-        def _():
-            a2a(lax.rem(me + shift + k - 1, n), me).start()
-
+        send_block(lax.rem(me + shift + k - 1, n))
         return carry
 
     lax.fori_loop(1, n, ratio_step, 0)
-    a2a(lax.rem(me + shift + n - 1, n), me).start()
+    send_block(lax.rem(me + shift + n - 1, n))
 
     dose_copy.wait()
     dstat[:, rows:] = jnp.zeros((16, SPILL), jnp.float32)
@@ -124,7 +168,6 @@
     @pl.when(has_next)
     def _():
         fwd(expr_ref, halo_expr, n).start()
-        fwd(sendbuf.at[me], halo.at[me], me).start()
 
     def relay(k, carry):
         source = lax.rem(me + 2 * n - shift - k, n)
@@ -133,7 +176,7 @@
         def _():
             a2a(source, source).wait_recv()
 
-            @pl.when(has_next)
+            @pl.when(jnp.logical_and(has_next, relayed(source, me)))
             def _():
                 fwd(recv.at[source], halo.at[source], source).start()
 
@@ -152,22 +195,7 @@
         stat[0] = lane_tiles_sum(value)
         stat[1] = lane_tiles_sum(value * value)
 
-    pack(recv, expr_ref, pheno, pstat)
-    pstat_pair = pair(1, pstat, pstat_in)
-
     dims = (((1,), (1,)), ((), ()))
-    prod[:, rows:] = jnp.zeros((all_rows, SPILL), jnp.float32)
-
-    def own_dot(k, carry):
-        at = pl.multiple_of(k * chunk, chunk)
-        prod[:, pl.ds(at, chunk)] = lax.dot_general(
-            pheno[...], dose[pl.ds(at, chunk), :], dims, preferred_element_type=jnp.float32
-        )
-        return carry
-
-    lax.fori_loop(0, rows // chunk, own_dot, 0)
-    pstat_pair.start()
-
     lane_gene = lax.broadcasted_iota(jnp.int32, (genes, LANE), 0)
     starts = jnp.zeros((genes, LANE), jnp.int32)
     for g in range(genes):
@@ -188,20 +216,6 @@
             picked.append(tile)
         return picked
 
-    def select_out(p, carry):
-        row = pl.multiple_of(p * genes, genes)
-        for t, tile in enumerate(windows(prod, row, other * width)):
-            sel_out[pl.ds(row, genes), t * LANE : (t + 1) * LANE] = tile
-        return carry
-
-    lax.fori_loop(0, phen, select_out, 0)
-    sel_pair = pair(2, sel_out, sel_in)
-    sel_pair.start()
-
-    dstat_pair.wait_recv()
-    dstat_pair.wait_send()
-    dstat[...] = dstat[...] + dstat_in[...]
-
     def scales(stat, stat_in, row):
         total = jnp.sum(stat[0, pl.ds(row, genes), :] + stat_in[0, pl.ds(row, genes), :], axis=1, keepdims=True)
         square = jnp.sum(stat[1, pl.ds(row, genes), :] + stat_in[1, pl.ds(row, genes), :], axis=1, keepdims=True)
@@ -222,10 +236,14 @@
         fwd(expr_ref, halo_expr, n).wait_recv()
 
         def arrive(k, carry):
-            fwd(recv.at[k], halo.at[k], k).wait_recv()
+            @pl.when(k != me)
+            def _():
+                fwd(recv.at[k], halo.at[k], k).wait_recv()
+
             return carry
 
         lax.fori_loop(0, n, arrive, 0)
+        halo[me] = sendbuf[lax.rem(me + n - 1, n)]
         pack(halo, halo_expr, hpheno, hstat)
 
         def halo_dot(k, carry):
@@ -238,6 +256,53 @@
         lax.fori_loop(0, 2, halo_dot, 0)
         hstat_pair.start()
         hprod_pair.start()
+
+    pack(recv, expr_ref, pheno, pstat)
+    pstat_pair = pair(1, pstat, pstat_in)
+
+    prod[:, rows:] = jnp.zeros((all_rows, SPILL), jnp.float32)
+
+    def own_dot(k, carry):
+        at = pl.multiple_of(k * chunk, chunk)
+        prod[:, pl.ds(at, chunk)] = lax.dot_general(
+            pheno[...], dose[pl.ds(at, chunk), :], dims, preferred_element_type=jnp.float32
+        )
+        return carry
+
+    lax.fori_loop(0, rows // chunk, own_dot, 0)
+    pstat_pair.start()
+
+    dstat_pair.wait_recv()
+    dstat_pair.wait_send()
+    dstat[...] = dstat[...] + dstat_in[...]
+
+    @pl.when(has_prev)
+    def _():
+        hstat_pair.wait_recv()
+        hprod_pair.wait_recv()
+        at = pl.multiple_of(core * half, half)
+        sums = dstat[0:8, pl.ds(at, half)]
+        scale = dose_scale(sums, dstat[8:16, pl.ds(at, half)])
+
+        def halo_out(p, carry):
+            row = pl.multiple_of(p * genes, genes)
+            mean, inv = scales(hstat, hstat_in, row)
+            cross = hprod[core, pl.ds(row, genes), :] + hprod_in[pl.ds(row, genes), :]
+            hres[p] = ((cross - sums * mean) * scale * inv).astype(jnp.bfloat16)
+            return carry
+
+        lax.fori_loop(0, phen, halo_out, 0)
+        back.start()
+
+    def select_out(p, carry):
+        row = pl.multiple_of(p * genes, genes)
+        for t, tile in enumerate(windows(prod, row, other * width)):
+            sel_out[pl.ds(row, genes), t * LANE : (t + 1) * LANE] = tile
+        return carry
+
+    lax.fori_loop(0, phen, select_out, 0)
+    sel_pair = pair(2, sel_out, sel_in)
+    sel_pair.start()
 
     pstat_pair.wait_recv()
     sel_pair.wait_recv()
@@ -248,24 +313,6 @@
         win[0:8, cols] = win_sum[t]
         win[8:16, cols] = dose_scale(win_sum[t], win_square[t])
 
-    @pl.when(has_prev)
-    def _():
-        hstat_pair.wait_recv()
-        hprod_pair.wait_recv()
-        at = pl.multiple_of(core * half, half)
-        sums = dstat[0:8, pl.ds(at, half)]
-        scale = dose_scale(sums, dstat[8:16, pl.ds(at, half)])
-
-        def halo_out(p, carry):
-            row = pl.multiple_of(p * genes, genes)
-            mean, inv = scales(hstat, hstat_in, row)
-            cross = hprod[core, pl.ds(row, genes), :] + hprod_in[pl.ds(row, genes), :]
-            hres[p] = ((cross - sums * mean) * scale * inv).astype(jnp.bfloat16)
-            return carry
-
-        lax.fori_loop(0, phen, halo_out, 0)
-        back.start()
-
     def own_out(p, carry):
         row = pl.multiple_of(p * genes, genes)
         mean, inv = scales(pstat, pstat_in, row)
@@ -323,6 +370,15 @@
         return carry
 
     lax.fori_loop(1, n, drain, 0)
+
+    def drain_ext(k, carry):
+        @pl.when(extends(k))
+        def _():
+            ext(k).wait_send()
+
+        return carry
+
+    lax.fori_loop(0, n, drain_ext, 0)
     pstat_pair.wait_send()
     sel_pair.wait_send()
 
@@ -331,7 +387,10 @@
         fwd(expr_ref, halo_expr, n).wait_send()
 
         def drain_fwd(k, carry):
-            fwd(recv.at[k], halo.at[k], k).wait_send()
+            @pl.when(relayed(k, me))
+            def _():
+                fwd(recv.at[k], halo.at[k], k).wait_send()
+
             return carry
 
         lax.fori_loop(0, n, drain_fwd, 0)
@@ -341,20 +400,6 @@
         hstat_pair.wait_send()
         hprod_pair.wait_send()
         back.wait_send()
-
-
-def mixing(cluster_sizes, valid_mask):
-    slots = valid_mask.shape[1]
-    clusters = cluster_sizes.shape[1]
-    slot = jnp.arange(slots, dtype=jnp.int32)
-    ends = []
-    for c in range(clusters):
-        ends.append(cluster_sizes[:, c] + (ends[-1] if c else 0))
-    cluster_id = sum((end[:, None] <= slot[None, :]).astype(jnp.int32) for end in ends)
-    same = cluster_id[:, :, None] == cluster_id[:, None, :]
-    diag = jnp.broadcast_to((slot[:, None] == slot[None, :])[None], same.shape)
-    both = jnp.concatenate([same, diag], axis=1)
-    return jnp.where(both, valid_mask[:, None, :], 0).astype(jnp.bfloat16)
 
 
 def shards(dosage, expression, intron_counts, cluster_sizes, valid_mask, gene_block, window_start):
@@ -367,8 +412,7 @@
     all_rows = phen * genes
     width = rows // 2
     half = SPILL // 2
-    counts_t = intron_counts.T.astype(jnp.float32).reshape(n * genes, slots, blk)
-    mix = mixing(cluster_sizes, valid_mask)
+    counts_t = intron_counts.T.reshape(n * genes, slots, blk)
     vmem = pl.BlockSpec(memory_space=pltpu.VMEM)
     smem = pl.BlockSpec(memory_space=pltpu.SMEM)
     f32, bf16 = jnp.float32, jnp.bfloat16
@@ -376,10 +420,11 @@
     result = pl.pallas_call(
         functools.partial(kernel, n, genes, slots),
         out_shape=jax.ShapeDtypeStruct((phen, genes, width), bf16),
-        in_specs=[smem, smem, vmem, vmem, vmem, pl.BlockSpec(memory_space=pl.ANY)],
+        in_specs=[smem, smem, vmem, vmem, vmem, vmem, pl.BlockSpec(memory_space=pl.ANY)],
         out_specs=vmem,
         scratch_shapes=[
             pltpu.VMEM((rows, samp), bf16),
+            pltpu.VMEM((n * genes, slots), jnp.int32),
             pltpu.VMEM((slots * genes, blk), f32),
             pltpu.VMEM((n, slots * genes, blk), bf16),
             pltpu.VMEM((n, slots * genes, blk), bf16),
@@ -404,12 +449,12 @@
             pltpu.VMEM((2, phen, genes, half), bf16),
             pltpu.VMEM((16, width), f32),
             dma, dma((n,)), dma((n,)), dma((n + 1,)), dma((n + 1,)), dma((5,)), dma((5,)),
-            dma, dma((2,)),
+            dma, dma((2,)), dma((n,)),
         ],
         compiler_params=pltpu.CompilerParams(
             collective_id=0, has_side_effects=True, vmem_limit_bytes=62 * 1024 * 1024
         ),
-    )(window_start, gene_block, counts_t, mix, expression, dosage)
+    )(window_start, gene_block, counts_t, cluster_sizes, valid_mask, expression, dosage)
     return jnp.transpose(result, (1, 0, 2))
 
 

time: 62.6 us -> 60.1 us (0.960)
  the two profiles are of different devices: /device:TPU:15 before, /device:TPU:1 now
where the time goes in v2:
time: 60.1 us; the launch traced here: 59.8 us
  Pallas kernels  52.9 us (88%)
  local copies, waits for them, and re-layouts  6.93 us (12%)
    pallas_call x1, Pallas kernels, shards(): pl.pallas_call(functools.partial(kernel, n, genes, slots), out_shape=jax....  52.9 us
    unnamed x3, local copies, waits for them, and re-layouts  4.76 us
    transpose x1, local copies, waits for them, and re-layouts, shards(): counts_t = intron_counts.T.reshape(n * genes, slots, blk)  2.16 us

profile of v2, /device:TPU:1, one launch (start us, length us, event | category | flops | bytes accessed | tf_op | source)
XLA Modules:
  0.0 59.8 jit_solution(16536735123762375925)
XLA Ops:
  0.0 1.4 %copy.9.sizes_ref = s32[64,8]{1,0:T(8,128)} copy(s32[64,8]{0,1:T(8,128)} %param.10) | data formatting | bytes 4096 | tf_op args[3]
  1.4 1.4 %copy.10.valid_ref = s32[64,40]{1,0:T(8,128)} copy(s32[64,40]{0,1:T(8,128)} %param.11) | data formatting | bytes 20480 | tf_op args[4]
  2.8 2.2 %copy.8 = bf16[2560,128]{1,0:T(8,128)(2,1)} copy(bf16[2560,128]{0,1:T(8,128)(2,1)} %bitcast.5) | data formatting | bytes 1310720 | tf_op jit(solution)/shard_map/transpose | solution.py:415
  5.0 52.9 %shard_map.73 = bf16[41,8,1024]{2,1,0:T(8,128)(2,1)} custom-call(s32[8]{0:T(128)} %starts_ref.1, s32[64]{0:T(128)} %block_ref.1, bf16[64,40,128]{2,1,0:T(8,128)(2,1)} %bitcast.4, s32[64,8]{1,0:T(8,128)} %copy.9.sizes_ref, s32[64,40]{1,0:T(8,128)} %copy.10.valid_ref, bf16[8,1024]{1,0:T(8,128)(2,1)} %expr_ref.1, bf16[2048,1024]{1,0:T(8,128)(2,1)} %dose_hbm.1), custom_call_target="tpu_custom_call" | custom-call | tf_op jit(solution)/shard_map/pallas_call | solution.py:420
  57.9 2.0 %copy.12 = bf16[8,41,1024]{2,0,1:T(8,128)(2,1)} copy(bf16[8,41,1024]{2,0,1:T(8,128)(2,1)} %bitcast.3) | data formatting | bytes 1343488

commit v3 on v2

--- a/solution.py
+++ b/solution.py
@@ -1,4 +1,5 @@
 import functools
+import math
 
 import jax
 import jax.numpy as jnp
@@ -21,7 +22,7 @@
 
 def kernel(
     n, genes, slots, starts_ref, block_ref, counts_ref, sizes_ref, valid_ref, expr_ref, dose_hbm, out_ref,
-    dose, ids, stage, sendbuf, recv, halo, halo_expr, pheno, hpheno, prod, hprod, hprod_in,
+    dose, ids, counts_t, stage, sendbuf, recv, halo, halo_expr, pheno, hpheno, prod, hprod, hprod_in,
     sel_out, sel_in, own_res, halo_full, dstat, dstat_in, pstat, pstat_in, hstat, hstat_in,
     hres, hres_in, win, dose_sem, a2a_send, a2a_recv, fwd_send, fwd_recv, pair_send, pair_recv,
     back_send, back_recv, ext_send,
@@ -35,7 +36,7 @@
     half = SPILL // 2
     intron_rows = slots * genes
     all_rows = phen * genes
-    blk = counts_ref.shape[2]
+    blk = counts_ref.shape[0]
     count = float(2 * samp)
     shift = n // 2
 
@@ -64,14 +65,25 @@
             device_id={"genes": owner}, device_id_type=MESH,
         )
 
-    slot_at = lax.broadcasted_iota(jnp.int32, ids.shape, 1)
-    end = jnp.zeros((ids.shape[0], 1), jnp.int32)
-    cluster_of = jnp.zeros(ids.shape, jnp.int32)
-    for c in range(sizes_ref.shape[1]):
-        end = end + sizes_ref[:, c : c + 1]
+    clusters = sizes_ref.shape[0]
+    slot_at = lax.broadcasted_iota(jnp.int32, valid_ref.shape, 0)
+    end = jnp.zeros((1, valid_ref.shape[1]), jnp.int32)
+    cluster_of = jnp.zeros(valid_ref.shape, jnp.int32)
+    for c in range(clusters):
+        end = end + sizes_ref[c : c + 1, :]
         cluster_of = cluster_of + (end <= slot_at).astype(jnp.int32)
-    ids[...] = cluster_of
-    clusters = sizes_ref.shape[1]
+    ids[0] = cluster_of.astype(jnp.float32).T
+    ids[1] = valid_ref[...].astype(jnp.float32).T
+    group = math.lcm(slots, LANE)
+    per = group // slots
+
+    def turn(k, carry):
+        at = pl.multiple_of(k * group, group)
+        piece = counts_ref[:, pl.ds(at, group)].astype(jnp.float32)
+        counts_t[pl.ds(k * per, per)] = piece.T.reshape(per, slots, blk)
+        return carry
+
+    lax.fori_loop(0, counts_ref.shape[1] // group, turn, 0)
     cluster_row = lax.broadcasted_iota(jnp.int32, (clusters, slots), 0)
     on_diagonal = lax.broadcasted_iota(jnp.int32, (slots, slots), 0) == lax.broadcasted_iota(
         jnp.int32, (slots, slots), 1
@@ -80,9 +92,9 @@
     def make_block(owner):
         for g in range(genes):
             gene = owner * genes + g
-            cnt = counts_ref[block_ref[gene]]
-            valid = valid_ref[pl.ds(gene, 1), :].astype(jnp.float32)
-            member = (cluster_row == ids[pl.ds(gene, 1), :]).astype(jnp.float32)
+            cnt = counts_t[block_ref[gene]].astype(jnp.bfloat16)
+            valid = ids[1, pl.ds(gene, 1), :]
+            member = (cluster_row == ids[0, pl.ds(gene, 1), :].astype(jnp.int32)).astype(jnp.float32)
             same = lax.dot_general(
                 member.astype(jnp.bfloat16), (member * valid).astype(jnp.bfloat16),
                 (((0,), (0,)), ((), ())), preferred_element_type=jnp.float32,
@@ -111,15 +123,18 @@
         far = jnp.logical_and(owner != n - 1, owner + 1 != me)
         return jnp.logical_and(far, jnp.logical_not(relayed(me, owner)))
 
+    def early(source, owner):
+        return jnp.logical_and(owner != n - 1, relayed(source, owner))
+
     def send_block(owner):
-        @pl.when(owner != me)
-        def _():
-            a2a(owner, me).start()
-
         @pl.when(extends(owner))
         def _():
             ext(owner).start()
 
+        @pl.when(early(me, owner))
+        def _():
+            a2a(owner, me).start()
+
     make_block(lax.rem(me + shift, n))
     pl.semaphore_wait(barrier, 2 * n - 1)
 
@@ -131,6 +146,17 @@
 
     lax.fori_loop(1, n, ratio_step, 0)
     send_block(lax.rem(me + shift + n - 1, n))
+
+    def late_step(k, carry):
+        owner = lax.rem(me + k, n)
+
+        @pl.when(jnp.logical_not(early(me, owner)))
+        def _():
+            a2a(owner, me).start()
+
+        return carry
+
+    lax.fori_loop(1, n, late_step, 0)
 
     dose_copy.wait()
     dstat[:, rows:] = jnp.zeros((16, SPILL), jnp.float32)
@@ -172,20 +198,25 @@
     def relay(k, carry):
         source = lax.rem(me + 2 * n - shift - k, n)
 
-        @pl.when(k != n - shift)
+        @pl.when(early(source, me))
         def _():
             a2a(source, source).wait_recv()
-
-            @pl.when(jnp.logical_and(has_next, relayed(source, me)))
-            def _():
-                fwd(recv.at[source], halo.at[source], source).start()
+            fwd(recv.at[source], halo.at[source], source).start()
+
+        return carry
+
+    def own_arrive(k, carry):
+        source = lax.rem(me + k, n)
+
+        @pl.when(jnp.logical_not(early(source, me)))
+        def _():
+            a2a(source, source).wait_recv()
 
         return carry
 
     dstat_pair = pair(0, dstat, dstat_in)
     dstat_pair.start()
     lax.fori_loop(0, n, relay, 0)
-    recv[me] = sendbuf[me]
 
     def pack(blocks, expr_rows, target, stat):
         for i in range(n):
@@ -257,21 +288,6 @@
         hstat_pair.start()
         hprod_pair.start()
 
-    pack(recv, expr_ref, pheno, pstat)
-    pstat_pair = pair(1, pstat, pstat_in)
-
-    prod[:, rows:] = jnp.zeros((all_rows, SPILL), jnp.float32)
-
-    def own_dot(k, carry):
-        at = pl.multiple_of(k * chunk, chunk)
-        prod[:, pl.ds(at, chunk)] = lax.dot_general(
-            pheno[...], dose[pl.ds(at, chunk), :], dims, preferred_element_type=jnp.float32
-        )
-        return carry
-
-    lax.fori_loop(0, rows // chunk, own_dot, 0)
-    pstat_pair.start()
-
     dstat_pair.wait_recv()
     dstat_pair.wait_send()
     dstat[...] = dstat[...] + dstat_in[...]
@@ -293,6 +309,23 @@
 
         lax.fori_loop(0, phen, halo_out, 0)
         back.start()
+
+    lax.fori_loop(1, n, own_arrive, 0)
+    recv[me] = sendbuf[me]
+    pack(recv, expr_ref, pheno, pstat)
+    pstat_pair = pair(1, pstat, pstat_in)
+
+    prod[:, rows:] = jnp.zeros((all_rows, SPILL), jnp.float32)
+
+    def own_dot(k, carry):
+        at = pl.multiple_of(k * chunk, chunk)
+        prod[:, pl.ds(at, chunk)] = lax.dot_general(
+            pheno[...], dose[pl.ds(at, chunk), :], dims, preferred_element_type=jnp.float32
+        )
+        return carry
+
+    lax.fori_loop(0, rows // chunk, own_dot, 0)
+    pstat_pair.start()
 
     def select_out(p, carry):
         row = pl.multiple_of(p * genes, genes)
@@ -412,7 +445,6 @@
     all_rows = phen * genes
     width = rows // 2
     half = SPILL // 2
-    counts_t = intron_counts.T.reshape(n * genes, slots, blk)
     vmem = pl.BlockSpec(memory_space=pltpu.VMEM)
     smem = pl.BlockSpec(memory_space=pltpu.SMEM)
     f32, bf16 = jnp.float32, jnp.bfloat16
@@ -424,7 +456,8 @@
         out_specs=vmem,
         scratch_shapes=[
             pltpu.VMEM((rows, samp), bf16),
-            pltpu.VMEM((n * genes, slots), jnp.int32),
+            pltpu.VMEM((2, n * genes, slots), f32),
+            pltpu.VMEM((n * genes, slots, blk), f32),
             pltpu.VMEM((slots * genes, blk), f32),
             pltpu.VMEM((n, slots * genes, blk), bf16),
             pltpu.VMEM((n, slots * genes, blk), bf16),
@@ -454,7 +487,7 @@
         compiler_params=pltpu.CompilerParams(
             collective_id=0, has_side_effects=True, vmem_limit_bytes=62 * 1024 * 1024
         ),
-    )(window_start, gene_block, counts_t, cluster_sizes, valid_mask, expression, dosage)
+    )(window_start, gene_block, intron_counts, cluster_sizes.T, valid_mask.T, expression, dosage)
     return jnp.transpose(result, (1, 0, 2))
 
 

time: 60.1 us -> 56.9 us (0.947)
  the two profiles are of different devices: /device:TPU:1 before, /device:TPU:11 now
where the time goes in v3:
time: 56.9 us; the launch traced here: 56.7 us
  Pallas kernels  54.7 us (96%)
  local copies, waits for them, and re-layouts  1.98 us (3%)
    pallas_call x1, Pallas kernels, shards(): pl.pallas_call(functools.partial(kernel, n, genes, slots), out_shape=jax....  54.7 us
    unnamed x1, local copies, waits for them, and re-layouts  1.98 us

profile of v3, /device:TPU:11, one launch (start us, length us, event | category | flops | bytes accessed | tf_op | source)
XLA Modules:
  0.0 56.7 jit_solution(4824950628401440067)
XLA Ops:
  0.0 54.7 %shard_map.73 = bf16[41,8,1024]{2,1,0:T(8,128)(2,1)} custom-call(s32[8]{0:T(128)} %starts_ref.1, s32[64]{0:T(128)} %block_ref.1, bf16[128,2560]{1,0:T(8,128)(2,1)} %counts_ref.1, s32[8,64]{1,0:T(8,128)} %bitcast.5, s32[40,64]{1,0:T(8,128)} %bitcast.4, bf16[8,1024]{1,0:T(8,128)(2,1)} %expr_ref.1, bf16[2048,1024]{1,0:T(8,128)(2,1)} %dose_hbm.1), custom_call_target="tpu_custom_call" | custom-call | tf_op jit(solution)/shard_map/pallas_call | solution.py:452
  54.7 2.0 %copy.9 = bf16[8,41,1024]{2,0,1:T(8,128)(2,1)} copy(bf16[8,41,1024]{2,0,1:T(8,128)(2,1)} %bitcast.3) | data formatting | bytes 1343488

commit v4 on v3

--- a/solution.py
+++ b/solution.py
@@ -131,7 +131,7 @@
         def _():
             ext(owner).start()
 
-        @pl.when(early(me, owner))
+        @pl.when(owner != me)
         def _():
             a2a(owner, me).start()
 
@@ -146,17 +146,6 @@
 
     lax.fori_loop(1, n, ratio_step, 0)
     send_block(lax.rem(me + shift + n - 1, n))
-
-    def late_step(k, carry):
-        owner = lax.rem(me + k, n)
-
-        @pl.when(jnp.logical_not(early(me, owner)))
-        def _():
-            a2a(owner, me).start()
-
-        return carry
-
-    lax.fori_loop(1, n, late_step, 0)
 
     dose_copy.wait()
     dstat[:, rows:] = jnp.zeros((16, SPILL), jnp.float32)

time: 56.9 us -> 55.7 us (0.979)
  Pallas kernels: 54.7 us -> 53.5 us
    pallas_call x1, Pallas kernels: 54.7 us -> 53.5 us  [shards(): pl.pallas_call(functools.partial(kernel, n, genes, slots), out_shape=jax....]
where the time goes in v4:
time: 55.7 us; the launch traced here: 55.5 us
  Pallas kernels  53.5 us (96%)
  local copies, waits for them, and re-layouts  1.98 us (4%)
    pallas_call x1, Pallas kernels, shards(): pl.pallas_call(functools.partial(kernel, n, genes, slots), out_shape=jax....  53.5 us
    unnamed x1, local copies, waits for them, and re-layouts  1.98 us

profile of v4, /device:TPU:11, one launch (start us, length us, event | category | flops | bytes accessed | tf_op | source)
XLA Modules:
  0.0 55.5 jit_solution(12956377363197298986)
XLA Ops:
  0.0 53.5 %shard_map.73 = bf16[41,8,1024]{2,1,0:T(8,128)(2,1)} custom-call(s32[8]{0:T(128)} %starts_ref.1, s32[64]{0:T(128)} %block_ref.1, bf16[128,2560]{1,0:T(8,128)(2,1)} %counts_ref.1, s32[8,64]{1,0:T(8,128)} %bitcast.5, s32[40,64]{1,0:T(8,128)} %bitcast.4, bf16[8,1024]{1,0:T(8,128)(2,1)} %expr_ref.1, bf16[2048,1024]{1,0:T(8,128)(2,1)} %dose_hbm.1), custom_call_target="tpu_custom_call" | custom-call | tf_op jit(solution)/shard_map/pallas_call | solution.py:441
  53.5 2.0 %copy.9 = bf16[8,41,1024]{2,0,1:T(8,128)(2,1)} copy(bf16[8,41,1024]{2,0,1:T(8,128)(2,1)} %bitcast.3) | data formatting | bytes 1343488
